TPU v7x, 512 devices: a whole 4x8x8 slice. The times are simulated.
512 devices in a mesh: gx: 128 (over z, y, core), gy: 4 (over x).
Axes of the slice: x: 4, y: 8, z: 8, core: 2. Of those that a mesh axis runs over, the one named last changes fastest.
Arguments:
- anomalies: float32 [80, 256, 32, 128], P(None, 'gx', 'gy'), may hold values from -6 to 6
- state_mean: float32 [256, 32, 128], P('gx', 'gy'), may hold values from -6 to 6
- obs_value: float32 [16, 256], P(None, 'gy'), may hold values from -8 to 8
- obs_cell: int32 [16, 256], replicated, may hold values from 0 to 2047
- owner: int32 [16], replicated, may hold values from 0 to 127, as said below
- order: int32 [16], replicated, may hold values from 0 to 15, each once
- root_inv: float32 [16, 256, 256], P(None, 'gy'), as said below
- gain_inv: float32 [16, 256, 256], P(None, 'gy'), as said below
Outputs:
- post_anomalies: float32 [80, 256, 32, 128], P(None, 'gx', 'gy')
- post_mean: float32 [256, 32, 128], P('gx', 'gy')
Inputs may be any that keep to these rules, and one draw needn't show every extreme that they name: `owner`: some batch lies at slab 128 - 2, some at slab 1 and some at slab 128 // 2; the others favour low slabs. `order`: each batch number once. `root_inv`: symmetric. `gain_inv`: symmetric.
All inputs are finite; a program needn't handle non-finite values.
Results may differ from a plain program's by a relative error of at most 0.0001.
Values sent between devices are 32-bit elements; how exact they have to be, the bound alone decides.
A program may use at most 64 MiB of HBM per device.

v0:
```python
import jax
import jax.numpy as jnp
from jax import lax
from jax.sharding import PartitionSpec as P

BATCHES = 16
REACH = 3


def shifted(value, axis, steps):
    count = lax.axis_size(axis)
    pairs = [(source, (source + steps) % count) for source in range(count)]
    return lax.ppermute(value, axis, pairs)


def gather_turned(arrays, axis, dims):
    turned = [jnp.moveaxis(a, dim, 0) for a, dim in zip(arrays, dims)]
    both = jnp.concatenate([t.reshape(len(t), -1) for t in turned], axis=1)
    out, at, done = (lax.all_gather(both, axis, axis=0, tiled=True), 0, [])
    for t, dim in zip(turned, dims):
        slab = out[:, at : at + t[0].size].reshape(-1, *t.shape[1:])
        done.append(jnp.moveaxis(slab, 0, dim))
        at += t[0].size
    return tuple(done)


def product(left_side, right_side):
    return jnp.dot(
        left_side, right_side, precision=lax.Precision.HIGHEST, preferred_element_type=jnp.float32
    )


def prior_relay(masked):
    total = masked
    upward = masked
    downward = masked
    for step in range(REACH):
        upward = shifted(upward, "gx", 1)
        downward = shifted(downward, "gx", -1)
        total = total + upward + downward
    return total


def local(anomalies, state_mean, obs_value, obs_cell, owner, order, root_inv, gain_inv):
    members, lon_dev, lat_dev, levels = anomalies.shape
    cell_count = lon_dev * lat_dev * levels
    quarter = obs_value.shape[1]
    obs_total = obs_cell.shape[1]
    slab_count = lax.axis_size("gx")
    band_count = lax.axis_size("gy")
    column = lax.axis_index("gx")
    band_index = lax.axis_index("gy")
    lon_total = slab_count * lon_dev
    lat_total = band_count * lat_dev
    taper_span = REACH * lon_dev + 1.0
    cell_ids = jnp.arange(cell_count, dtype=jnp.int32)
    cell_lon = column * lon_dev + cell_ids // (lat_dev * levels)
    cell_lat = band_index * lat_dev + cell_ids // levels % lat_dev
    obs_band = jnp.arange(obs_total, dtype=jnp.int32) // quarter

    def assimilate(batch_turn, carried):
        state_rows, mean_row = carried
        batch_id = order[batch_turn]
        root_slab = owner[batch_id]
        is_root = column == root_slab
        cells_of = obs_cell[batch_id]
        local_ids = lax.dynamic_slice_in_dim(cells_of, band_index * quarter, quarter)
        picked = jnp.take(state_rows, local_ids, axis=1)
        innovation = obs_value[batch_id] - jnp.take(mean_row, local_ids)
        root_rows = root_inv[batch_id]
        gain_rows = gain_inv[batch_id]
        joined = jnp.concatenate([picked, innovation[None, :]], axis=0)
        masked = jnp.where(is_root, joined, jnp.zeros_like(joined))
        joined = prior_relay(masked)
        picked, innovation = (joined[:members], joined[members])
        prior_all, innov_all = gather_turned((picked, innovation), "gy", (1, 0))
        weighted = product(prior_all, root_rows.T)
        gain_part = product(gain_rows, innov_all)
        weighted_all, gain_all = gather_turned((weighted, gain_part), "gy", (1, 0))
        obs_lon = root_slab * lon_dev + cells_of // (lat_dev * levels)
        obs_lat = obs_band * lat_dev + cells_of // levels % lat_dev
        slab_gap = jnp.abs(column - root_slab)
        in_reach = jnp.minimum(slab_gap, slab_count - slab_gap) <= REACH

        def near_update(operands):
            rows_now, mean_now = operands
            lon_gap = jnp.abs(obs_lon[:, None] - cell_lon[None, :])
            cycle_gap = jnp.minimum(lon_gap, lon_total - lon_gap)
            lat_gap = jnp.abs(obs_lat[:, None] - cell_lat[None, :])
            taper_rows = jnp.maximum(0.0, 1.0 - cycle_gap.astype(jnp.float32) / taper_span) * (
                1.0 - lat_gap.astype(jnp.float32) / lat_total
            )
            covariance = product(prior_all.T, rows_now) / (members - 1.0)
            gained = taper_rows * covariance
            stacked = jnp.concatenate([weighted_all, gain_all[None, :]], axis=0)
            increment = product(stacked, gained)
            return (rows_now - increment[:members], mean_now + increment[members])

        def keep_all(operands):
            return operands

        return lax.cond(in_reach, near_update, keep_all, (state_rows, mean_row))

    start_rows = anomalies.reshape(members, cell_count)
    start_mean = state_mean.reshape(cell_count)
    final_rows, final_mean = lax.fori_loop(0, BATCHES, assimilate, (start_rows, start_mean))
    return (
        final_rows.reshape(members, lon_dev, lat_dev, levels),
        final_mean.reshape(lon_dev, lat_dev, levels),
    )


def solution(mesh):
    return jax.shard_map(
        local,
        mesh=mesh,
        in_specs=(
            P(None, "gx", "gy", None),
            P("gx", "gy", None),
            P(None, "gy"),
            P(),
            P(),
            P(),
            P(None, "gy", None),
            P(None, "gy", None),
        ),
        out_specs=(P(None, "gx", "gy", None), P("gx", "gy", None)),
        check_vma=False,
    )
```

profile of v0, /device:TPU:2, one launch (start us, length us, event | category | flops | bytes accessed | tf_op | source)
XLA Modules:
  0.0 1054.0 jit_solution(2086697936089289550)
XLA Ops:
  3.4 1049.5 %while.19 = (s32[]{:T(128)}, f32[80,2048]{1,0:T(8,128)S(1)}, f32[2048]{0:T(1024)S(1)}, s32[16]{0:T(128)}, s32[16]{0:T(128)}, /*index=5*/s32[]{:T(128)}, s32[16,2...) while((s32[]{:T(128)}, f32[80,2048]{1,0:T(8,128)S(1)}, ...), condition=%wide.region_3.4_spmd.clone, body=%wide.region_0.3_spmd.clone.sunk | while | flops 1037565760 | bytes 11027220 | solution.py:106
  13.8 13.3 %collective-permute-start = (f32[81,64]{0,1:T(8,128)S(1)}, f32[81,64]{0,1:T(8,128)S(1)}, u32[]{:S(2)}, u32[]{:S(2)}) collective-permute-start(f32[81,64]{0,1:T(8,128)S(1)} %maximum_select_fusion.2), channel_id=1, source_target_pairs={{0,508},{4,0},{8,4},{12,8},{16,12},{20,16},{24,20},{28,24},{32,28}... | collective-permute-start | bytes 62216 | tf_op jit(solution)/shard_map/while/body/eval_jaxpr/ppermute | solution.py:13
  29.1 7.0 collective-permute-start.1
  38.0 7.0 collective-permute-start.2
  46.8 12.0 %all_gather.26 = f32[256,81]{1,0:T(8,128)S(1)} all-gather(f32[64,81]{1,0:T(8,128)S(1)} %pad_maximum_fusion.4), channel_id=1, replica_groups=mesh['gx'=128,'gy'=4] {'gy'}, dimensions={0}, use_global_device_ids=true | all-gather | bytes 103680 | tf_op jit(solution)/shard_map/while/body/eval_jaxpr/all_gather | solution.py:19
  61.2 12.0 %all_gather.27 = f32[256,81]{1,0:T(8,128)S(1)} all-gather(f32[64,81]{1,0:T(8,128)S(1)} %pad_maximum_fusion.5), channel_id=1, replica_groups=mesh['gx'=128,'gy'=4] {'gy'}, dimensions={0}, use_global_device_ids=true | all-gather | bytes 103680 | tf_op jit(solution)/shard_map/while/body/eval_jaxpr/all_gather | solution.py:19
  83.7 7.0 collective-permute-start
  92.6 7.0 collective-permute-start.1
  101.5 7.0 collective-permute-start.2
  110.3 12.0 %all_gather.26 = f32[256,81]{1,0:T(8,128)S(1)} all-gather(f32[64,81]{1,0:T(8,128)S(1)} %pad_maximum_fusion.4), channel_id=1, replica_groups=mesh['gx'=128,'gy'=4] {'gy'}, dimensions={0}, use_global_device_ids=true | all-gather | bytes 103680 | tf_op jit(solution)/shard_map/while/body/eval_jaxpr/all_gather | solution.py:19
  124.7 12.0 %all_gather.27 = f32[256,81]{1,0:T(8,128)S(1)} all-gather(f32[64,81]{1,0:T(8,128)S(1)} %pad_maximum_fusion.5), channel_id=1, replica_groups=mesh['gx'=128,'gy'=4] {'gy'}, dimensions={0}, use_global_device_ids=true | all-gather | bytes 103680 | tf_op jit(solution)/shard_map/while/body/eval_jaxpr/all_gather | solution.py:19
  152.7 7.0 collective-permute-start
  161.6 7.0 collective-permute-start.1
  170.5 7.0 collective-permute-start.2
  179.3 12.0 %all_gather.26 = f32[256,81]{1,0:T(8,128)S(1)} all-gather(f32[64,81]{1,0:T(8,128)S(1)} %pad_maximum_fusion.4), channel_id=1, replica_groups=mesh['gx'=128,'gy'=4] {'gy'}, dimensions={0}, use_global_device_ids=true | all-gather | bytes 103680 | tf_op jit(solution)/shard_map/while/body/eval_jaxpr/all_gather | solution.py:19
  193.7 12.0 %all_gather.27 = f32[256,81]{1,0:T(8,128)S(1)} all-gather(f32[64,81]{1,0:T(8,128)S(1)} %pad_maximum_fusion.5), channel_id=1, replica_groups=mesh['gx'=128,'gy'=4] {'gy'}, dimensions={0}, use_global_device_ids=true | all-gather | bytes 103680 | tf_op jit(solution)/shard_map/while/body/eval_jaxpr/all_gather | solution.py:19
  216.1 7.0 collective-permute-start
  225.1 7.0 collective-permute-start.1
  234.0 7.0 collective-permute-start.2
  242.8 12.0 %all_gather.26 = f32[256,81]{1,0:T(8,128)S(1)} all-gather(f32[64,81]{1,0:T(8,128)S(1)} %pad_maximum_fusion.4), channel_id=1, replica_groups=mesh['gx'=128,'gy'=4] {'gy'}, dimensions={0}, use_global_device_ids=true | all-gather | bytes 103680 | tf_op jit(solution)/shard_map/while/body/eval_jaxpr/all_gather | solution.py:19
  257.1 12.0 %all_gather.27 = f32[256,81]{1,0:T(8,128)S(1)} all-gather(f32[64,81]{1,0:T(8,128)S(1)} %pad_maximum_fusion.5), channel_id=1, replica_groups=mesh['gx'=128,'gy'=4] {'gy'}, dimensions={0}, use_global_device_ids=true | all-gather | bytes 103680 | tf_op jit(solution)/shard_map/while/body/eval_jaxpr/all_gather | solution.py:19
  285.2 7.0 collective-permute-start
  294.1 7.0 collective-permute-start.1
  303.0 7.0 collective-permute-start.2
  311.8 12.0 %all_gather.26 = f32[256,81]{1,0:T(8,128)S(1)} all-gather(f32[64,81]{1,0:T(8,128)S(1)} %pad_maximum_fusion.4), channel_id=1, replica_groups=mesh['gx'=128,'gy'=4] {'gy'}, dimensions={0}, use_global_device_ids=true | all-gather | bytes 103680 | tf_op jit(solution)/shard_map/while/body/eval_jaxpr/all_gather | solution.py:19
  326.2 12.0 %all_gather.27 = f32[256,81]{1,0:T(8,128)S(1)} all-gather(f32[64,81]{1,0:T(8,128)S(1)} %pad_maximum_fusion.5), channel_id=1, replica_groups=mesh['gx'=128,'gy'=4] {'gy'}, dimensions={0}, use_global_device_ids=true | all-gather | bytes 103680 | tf_op jit(solution)/shard_map/while/body/eval_jaxpr/all_gather | solution.py:19
  348.6 7.0 collective-permute-start
  357.5 7.0 collective-permute-start.1
  366.5 7.0 collective-permute-start.2
  375.3 12.0 %all_gather.26 = f32[256,81]{1,0:T(8,128)S(1)} all-gather(f32[64,81]{1,0:T(8,128)S(1)} %pad_maximum_fusion.4), channel_id=1, replica_groups=mesh['gx'=128,'gy'=4] {'gy'}, dimensions={0}, use_global_device_ids=true | all-gather | bytes 103680 | tf_op jit(solution)/shard_map/while/body/eval_jaxpr/all_gather | solution.py:19
  389.6 12.0 %all_gather.27 = f32[256,81]{1,0:T(8,128)S(1)} all-gather(f32[64,81]{1,0:T(8,128)S(1)} %pad_maximum_fusion.5), channel_id=1, replica_groups=mesh['gx'=128,'gy'=4] {'gy'}, dimensions={0}, use_global_device_ids=true | all-gather | bytes 103680 | tf_op jit(solution)/shard_map/while/body/eval_jaxpr/all_gather | solution.py:19
  417.6 7.0 collective-permute-start
  426.6 7.0 collective-permute-start.1
  435.5 7.0 collective-permute-start.2
  444.3 12.0 %all_gather.26 = f32[256,81]{1,0:T(8,128)S(1)} all-gather(f32[64,81]{1,0:T(8,128)S(1)} %pad_maximum_fusion.4), channel_id=1, replica_groups=mesh['gx'=128,'gy'=4] {'gy'}, dimensions={0}, use_global_device_ids=true | all-gather | bytes 103680 | tf_op jit(solution)/shard_map/while/body/eval_jaxpr/all_gather | solution.py:19
  458.6 12.0 %all_gather.27 = f32[256,81]{1,0:T(8,128)S(1)} all-gather(f32[64,81]{1,0:T(8,128)S(1)} %pad_maximum_fusion.5), channel_id=1, replica_groups=mesh['gx'=128,'gy'=4] {'gy'}, dimensions={0}, use_global_device_ids=true | all-gather | bytes 103680 | tf_op jit(solution)/shard_map/while/body/eval_jaxpr/all_gather | solution.py:19
  481.1 7.0 collective-permute-start
  490.0 7.0 collective-permute-start.1
  498.9 7.0 collective-permute-start.2
  507.8 12.0 %all_gather.26 = f32[256,81]{1,0:T(8,128)S(1)} all-gather(f32[64,81]{1,0:T(8,128)S(1)} %pad_maximum_fusion.4), channel_id=1, replica_groups=mesh['gx'=128,'gy'=4] {'gy'}, dimensions={0}, use_global_device_ids=true | all-gather | bytes 103680 | tf_op jit(solution)/shard_map/while/body/eval_jaxpr/all_gather | solution.py:19
  522.1 12.0 %all_gather.27 = f32[256,81]{1,0:T(8,128)S(1)} all-gather(f32[64,81]{1,0:T(8,128)S(1)} %pad_maximum_fusion.5), channel_id=1, replica_groups=mesh['gx'=128,'gy'=4] {'gy'}, dimensions={0}, use_global_device_ids=true | all-gather | bytes 103680 | tf_op jit(solution)/shard_map/while/body/eval_jaxpr/all_gather | solution.py:19
  544.5 7.0 collective-permute-start
  553.5 7.0 collective-permute-start.1
  571.2 12.0 %all_gather.26 = f32[256,81]{1,0:T(8,128)S(1)} all-gather(f32[64,81]{1,0:T(8,128)S(1)} %pad_maximum_fusion.4), channel_id=1, replica_groups=mesh['gx'=128,'gy'=4] {'gy'}, dimensions={0}, use_global_device_ids=true | all-gather | bytes 103680 | tf_op jit(solution)/shard_map/while/body/eval_jaxpr/all_gather | solution.py:19
  585.6 12.0 %all_gather.27 = f32[256,81]{1,0:T(8,128)S(1)} all-gather(f32[64,81]{1,0:T(8,128)S(1)} %pad_maximum_fusion.5), channel_id=1, replica_groups=mesh['gx'=128,'gy'=4] {'gy'}, dimensions={0}, use_global_device_ids=true | all-gather | bytes 103680 | tf_op jit(solution)/shard_map/while/body/eval_jaxpr/all_gather | solution.py:19
  608.0 7.0 collective-permute-start
  625.9 7.0 collective-permute-start.2
  634.7 12.0 %all_gather.26 = f32[256,81]{1,0:T(8,128)S(1)} all-gather(f32[64,81]{1,0:T(8,128)S(1)} %pad_maximum_fusion.4), channel_id=1, replica_groups=mesh['gx'=128,'gy'=4] {'gy'}, dimensions={0}, use_global_device_ids=true | all-gather | bytes 103680 | tf_op jit(solution)/shard_map/while/body/eval_jaxpr/all_gather | solution.py:19
  649.0 12.0 %all_gather.27 = f32[256,81]{1,0:T(8,128)S(1)} all-gather(f32[64,81]{1,0:T(8,128)S(1)} %pad_maximum_fusion.5), channel_id=1, replica_groups=mesh['gx'=128,'gy'=4] {'gy'}, dimensions={0}, use_global_device_ids=true | all-gather | bytes 103680 | tf_op jit(solution)/shard_map/while/body/eval_jaxpr/all_gather | solution.py:19
  698.1 12.0 %all_gather.26 = f32[256,81]{1,0:T(8,128)S(1)} all-gather(f32[64,81]{1,0:T(8,128)S(1)} %pad_maximum_fusion.4), channel_id=1, replica_groups=mesh['gx'=128,'gy'=4] {'gy'}, dimensions={0}, use_global_device_ids=true | all-gather | bytes 103680 | tf_op jit(solution)/shard_map/while/body/eval_jaxpr/all_gather | solution.py:19
  712.5 12.0 %all_gather.27 = f32[256,81]{1,0:T(8,128)S(1)} all-gather(f32[64,81]{1,0:T(8,128)S(1)} %pad_maximum_fusion.5), channel_id=1, replica_groups=mesh['gx'=128,'gy'=4] {'gy'}, dimensions={0}, use_global_device_ids=true | all-gather | bytes 103680 | tf_op jit(solution)/shard_map/while/body/eval_jaxpr/all_gather | solution.py:19
  761.6 12.0 %all_gather.26 = f32[256,81]{1,0:T(8,128)S(1)} all-gather(f32[64,81]{1,0:T(8,128)S(1)} %pad_maximum_fusion.4), channel_id=1, replica_groups=mesh['gx'=128,'gy'=4] {'gy'}, dimensions={0}, use_global_device_ids=true | all-gather | bytes 103680 | tf_op jit(solution)/shard_map/while/body/eval_jaxpr/all_gather | solution.py:19
  775.9 12.0 %all_gather.27 = f32[256,81]{1,0:T(8,128)S(1)} all-gather(f32[64,81]{1,0:T(8,128)S(1)} %pad_maximum_fusion.5), channel_id=1, replica_groups=mesh['gx'=128,'gy'=4] {'gy'}, dimensions={0}, use_global_device_ids=true | all-gather | bytes 103680 | tf_op jit(solution)/shard_map/while/body/eval_jaxpr/all_gather | solution.py:19
  825.1 12.0 %all_gather.26 = f32[256,81]{1,0:T(8,128)S(1)} all-gather(f32[64,81]{1,0:T(8,128)S(1)} %pad_maximum_fusion.4), channel_id=1, replica_groups=mesh['gx'=128,'gy'=4] {'gy'}, dimensions={0}, use_global_device_ids=true | all-gather | bytes 103680 | tf_op jit(solution)/shard_map/while/body/eval_jaxpr/all_gather | solution.py:19
  839.4 12.0 %all_gather.27 = f32[256,81]{1,0:T(8,128)S(1)} all-gather(f32[64,81]{1,0:T(8,128)S(1)} %pad_maximum_fusion.5), channel_id=1, replica_groups=mesh['gx'=128,'gy'=4] {'gy'}, dimensions={0}, use_global_device_ids=true | all-gather | bytes 103680 | tf_op jit(solution)/shard_map/while/body/eval_jaxpr/all_gather | solution.py:19
  876.3 7.0 collective-permute-start.1
  894.1 12.0 %all_gather.26 = f32[256,81]{1,0:T(8,128)S(1)} all-gather(f32[64,81]{1,0:T(8,128)S(1)} %pad_maximum_fusion.4), channel_id=1, replica_groups=mesh['gx'=128,'gy'=4] {'gy'}, dimensions={0}, use_global_device_ids=true | all-gather | bytes 103680 | tf_op jit(solution)/shard_map/while/body/eval_jaxpr/all_gather | solution.py:19
  908.4 12.0 %all_gather.27 = f32[256,81]{1,0:T(8,128)S(1)} all-gather(f32[64,81]{1,0:T(8,128)S(1)} %pad_maximum_fusion.5), channel_id=1, replica_groups=mesh['gx'=128,'gy'=4] {'gy'}, dimensions={0}, use_global_device_ids=true | all-gather | bytes 103680 | tf_op jit(solution)/shard_map/while/body/eval_jaxpr/all_gather | solution.py:19
  957.5 12.0 %all_gather.26 = f32[256,81]{1,0:T(8,128)S(1)} all-gather(f32[64,81]{1,0:T(8,128)S(1)} %pad_maximum_fusion.4), channel_id=1, replica_groups=mesh['gx'=128,'gy'=4] {'gy'}, dimensions={0}, use_global_device_ids=true | all-gather | bytes 103680 | tf_op jit(solution)/shard_map/while/body/eval_jaxpr/all_gather | solution.py:19
  971.9 12.0 %all_gather.27 = f32[256,81]{1,0:T(8,128)S(1)} all-gather(f32[64,81]{1,0:T(8,128)S(1)} %pad_maximum_fusion.5), channel_id=1, replica_groups=mesh['gx'=128,'gy'=4] {'gy'}, dimensions={0}, use_global_device_ids=true | all-gather | bytes 103680 | tf_op jit(solution)/shard_map/while/body/eval_jaxpr/all_gather | solution.py:19
  994.3 7.0 collective-permute-start
  1012.2 7.0 collective-permute-start.2
  1021.0 12.0 %all_gather.26 = f32[256,81]{1,0:T(8,128)S(1)} all-gather(f32[64,81]{1,0:T(8,128)S(1)} %pad_maximum_fusion.4), channel_id=1, replica_groups=mesh['gx'=128,'gy'=4] {'gy'}, dimensions={0}, use_global_device_ids=true | all-gather | bytes 103680 | tf_op jit(solution)/shard_map/while/body/eval_jaxpr/all_gather | solution.py:19
  1035.3 12.0 %all_gather.27 = f32[256,81]{1,0:T(8,128)S(1)} all-gather(f32[64,81]{1,0:T(8,128)S(1)} %pad_maximum_fusion.5), channel_id=1, replica_groups=mesh['gx'=128,'gy'=4] {'gy'}, dimensions={0}, use_global_device_ids=true | all-gather | bytes 103680 | tf_op jit(solution)/shard_map/while/body/eval_jaxpr/all_gather | solution.py:19
  (761 shorter events, 413.0 us)
Async XLA Ops:
  11.9 15.2 %collective-permute-start.3 = (f32[81,64]{0,1:T(8,128)S(1)}, f32[81,64]{0,1:T(8,128)S(1)}, u32[]{:S(2)}, u32[]{:S(2)}) collective-permute-start(f32[81,64]{0,1:T(8,128)S(1)} %maximum_select_fusion.2), channel_id=1, source_target_pairs={{0,4},{4,8},{8,12},{12,16},{16,20},{20,24},{24,28},{28,32},{32,36}... | collective-permute-start | bytes 62216 | tf_op jit(solution)/shard_map/while/body/eval_jaxpr/ppermute | solution.py:13
  13.8 15.3 %collective-permute-start = (f32[81,64]{0,1:T(8,128)S(1)}, f32[81,64]{0,1:T(8,128)S(1)}, u32[]{:S(2)}, u32[]{:S(2)}) collective-permute-start(f32[81,64]{0,1:T(8,128)S(1)} %maximum_select_fusion.2), channel_id=1, source_target_pairs={{0,508},{4,0},{8,4},{12,8},{16,12},{20,16},{24,20},{28,24},{32,28}... | collective-permute-start | bytes 62216 | tf_op jit(solution)/shard_map/while/body/eval_jaxpr/ppermute | solution.py:13
  27.1 8.9 collective-permute-start.4
  29.1 8.9 collective-permute-start.1
  36.1 9.8 collective-permute-start.5
  83.7 8.9 collective-permute-start
  90.7 8.9 collective-permute-start.4
  92.6 8.9 collective-permute-start.1
  99.6 9.8 collective-permute-start.5
  152.7 8.9 collective-permute-start
  159.7 8.9 collective-permute-start.4
  161.6 8.9 collective-permute-start.1
  168.6 9.8 collective-permute-start.5
  216.1 8.9 collective-permute-start
  223.1 8.9 collective-permute-start.4
  225.1 8.9 collective-permute-start.1
  232.1 9.8 collective-permute-start.5
  285.2 8.9 collective-permute-start
  292.1 8.9 collective-permute-start.4
  294.1 8.9 collective-permute-start.1
  301.1 9.8 collective-permute-start.5
  348.6 8.9 collective-permute-start
  355.6 8.9 collective-permute-start.4
  357.5 8.9 collective-permute-start.1
  364.5 9.8 collective-permute-start.5
  417.6 8.9 collective-permute-start
  424.6 8.9 collective-permute-start.4
  426.6 8.9 collective-permute-start.1
  433.6 9.8 collective-permute-start.5
  481.1 8.9 collective-permute-start
  488.1 8.9 collective-permute-start.4
  490.0 8.9 collective-permute-start.1
  497.0 9.8 collective-permute-start.5
  544.5 8.9 collective-permute-start
  551.5 8.9 collective-permute-start.4
  553.5 8.9 collective-permute-start.1
  560.5 9.8 collective-permute-start.5
  608.0 8.9 collective-permute-start
  615.0 8.9 collective-permute-start.4
  616.9 8.9 collective-permute-start.1
  623.9 9.8 collective-permute-start.5
  671.5 8.9 collective-permute-start
  678.5 8.9 collective-permute-start.4
  680.4 8.9 collective-permute-start.1
  687.4 9.8 collective-permute-start.5
  734.9 8.9 collective-permute-start
  741.9 8.9 collective-permute-start.4
  743.9 8.9 collective-permute-start.1
  750.9 9.8 collective-permute-start.5
  798.4 8.9 collective-permute-start
  805.4 8.9 collective-permute-start.4
  807.3 8.9 collective-permute-start.1
  814.3 9.8 collective-permute-start.5
  867.4 8.9 collective-permute-start
  874.4 8.9 collective-permute-start.4
  876.3 8.9 collective-permute-start.1
  883.3 9.8 collective-permute-start.5
  930.9 8.9 collective-permute-start
  937.9 8.9 collective-permute-start.4
  939.8 8.9 collective-permute-start.1
  946.8 9.8 collective-permute-start.5
  1001.3 8.9 collective-permute-start.4
  1003.3 8.9 collective-permute-start.1
  1010.3 9.8 collective-permute-start.5
  (33 other events, 280.3 us)
where the time goes:
time: 1060 us; the launch traced here: 1050 us
  starting transfers between devices  433 us (41%)
  blocking collectives  384 us (36%)
  local copies, waits for them, and re-layouts  98.4 us (9%)
  loops' own time  62.6 us (6%)
  matrix products  55.5 us (5%)
  waiting for transfers between devices  11.1 us (1%)
    ppermute x96, starting transfers between devices, shifted(): return lax.ppermute(value, axis, pairs)  433 us
    all_gather x32, blocking collectives, gather_turned(): out, at, done = (lax.all_gather(both, axis, axis=0, tiled=True), 0, [])  384 us
    another operation x1, loops' own time, local(): lax.fori_loop(0, BATCHES, assimilate, (start_rows, start_mean))  58.7 us
    dot_general x42, matrix products, product(): jnp.dot(left_side, right_side, precision=lax.Precision.HIGHEST, preferred...  55.5 us
  transfers between devices with their start and end apart: 96, of which 16 were waited for; matrix products, arithmetic and copies ran while one was open for 0% of the time, Pallas kernels for 0%

commit v1 on v0

--- a/solution.py
+++ b/solution.py
@@ -16,7 +16,13 @@
 def gather_turned(arrays, axis, dims):
     turned = [jnp.moveaxis(a, dim, 0) for a, dim in zip(arrays, dims)]
     both = jnp.concatenate([t.reshape(len(t), -1) for t in turned], axis=1)
-    out, at, done = (lax.all_gather(both, axis, axis=0, tiled=True), 0, [])
+    out, at, done = (
+        jnp.concatenate(
+            lax.all_to_all(jnp.stack([both] * lax.axis_size(axis), axis=0), axis, 0, 0), axis=0
+        ),
+        0,
+        [],
+    )
     for t, dim in zip(turned, dims):
         slab = out[:, at : at + t[0].size].reshape(-1, *t.shape[1:])
         done.append(jnp.moveaxis(slab, 0, dim))

time: 1060 us -> 991 us (0.935)
  blocking collectives: 384 us -> 0 us
  starting transfers between devices: 433 us -> 585 us
  waiting for transfers between devices: 11.1 us -> 158 us
  local copies, waits for them, and re-layouts: 98.4 us -> 118 us
    all_gather x32 -> x0, blocking collectives: 384 us -> none  [gather_turned(): out, at, done = (lax.all_gather(both, axis, axis=0, tiled=True), 0, [])]
    all_to_all x0 -> x32, starting transfers between devices: none -> 152 us  [gather_turned(): lax.all_to_all(jnp.stack([both] * lax.axis_size(axis), axis=0), axis, 0, 0)]
    all_to_all x0 -> x32, waiting for transfers between devices: none -> 145 us  [gather_turned(): lax.all_to_all(jnp.stack([both] * lax.axis_size(axis), axis=0), axis, 0, 0)]
    another operation x26 -> x58, local copies, waits for them, and re-layouts: 0.96 us -> 22.5 us  [the longest x32 21.5 us: gather_turned(): jnp.stack([both] * lax.axis_size(axis), axis=0)]
  transfers between devices with their start and end apart: 96 -> 128, of which waited for: 16 -> 48; matrix products, arithmetic and copies ran while one was open for 0% -> 0% of each run, Pallas kernels for 0% -> 0%
where the time goes in v1:
time: 991 us; the launch traced here: 982 us
  starting transfers between devices  585 us (59%)
  waiting for transfers between devices  158 us (16%)
  local copies, waits for them, and re-layouts  118 us (12%)
  loops' own time  56.3 us (6%)
  matrix products  55.5 us (6%)
    ppermute x96, starting transfers between devices, shifted(): return lax.ppermute(value, axis, pairs)  433 us
    all_to_all x32, starting transfers between devices, gather_turned(): lax.all_to_all(jnp.stack([both] * lax.axis_size(axis), axis=0), axis, 0, 0)  152 us
    all_to_all x32, waiting for transfers between devices, gather_turned(): lax.all_to_all(jnp.stack([both] * lax.axis_size(axis), axis=0), axis, 0, 0)  145 us
    dot_general x42, matrix products, product(): jnp.dot(left_side, right_side, precision=lax.Precision.HIGHEST, preferred...  55.5 us
    another operation x1, loops' own time, local(): lax.fori_loop(0, BATCHES, assimilate, (start_rows, start_mean))  53 us
    another operation x32, local copies, waits for them, and re-layouts, gather_turned(): jnp.stack([both] * lax.axis_size(axis), axis=0)  21.5 us
    dynamic_slice x16, local copies, waits for them, and re-layouts, assimilate(): root_slab = owner[batch_id]  19.9 us
    dynamic_slice x16, local copies, waits for them, and re-layouts, assimilate(): batch_id = order[batch_turn]  19.9 us
  transfers between devices with their start and end apart: 128, of which 48 were waited for; matrix products, arithmetic and copies ran while one was open for 0% of the time, Pallas kernels for 0%

profile of v1, /device:TPU:2, one launch (start us, length us, event | category | flops | bytes accessed | tf_op | source)
XLA Modules:
  0.0 982.0 jit_solution(991513052951710378)
XLA Ops:
  3.4 977.6 %while.19 = (s32[]{:T(128)}, f32[80,2048]{1,0:T(8,128)S(1)}, f32[2048]{0:T(1024)S(1)}, s32[16]{0:T(128)}, s32[16]{0:T(128)}, /*index=5*/s32[]{:T(128)}, s32[16,2...) while((s32[]{:T(128)}, f32[80,2048]{1,0:T(8,128)S(1)}, ...), condition=%wide.region_3.4_spmd.clone, body=%wide.region_0.3_spmd.clone.sunk | while | flops 1037565760 | bytes 11717460 | solution.py:112
  13.5 13.3 %collective-permute-start = (f32[81,64]{0,1:T(8,128)S(1)}, f32[81,64]{0,1:T(8,128)S(1)}, u32[]{:S(2)}, u32[]{:S(2)}) collective-permute-start(f32[81,64]{0,1:T(8,128)S(1)} %maximum_select_fusion.2), channel_id=1, source_target_pairs={{0,508},{4,0},{8,4},{12,8},{16,12},{20,16},{24,20},{28,24},{32,28}... | collective-permute-start | bytes 62216 | tf_op jit(solution)/shard_map/while/body/eval_jaxpr/ppermute | solution.py:13
  28.7 7.0 collective-permute-start.1
  37.6 7.0 collective-permute-start.2
  47.1 4.8 all-to-all-start
  59.5 4.8 all-to-all-start.1
  78.9 7.0 collective-permute-start
  87.8 7.0 collective-permute-start.1
  96.7 7.0 collective-permute-start.2
  127.8 5.5 conditional.3
  143.3 7.0 collective-permute-start
  152.2 7.0 collective-permute-start.1
  161.1 7.0 collective-permute-start.2
  182.9 4.8 all-to-all-start.1
  202.3 7.0 collective-permute-start
  211.2 7.0 collective-permute-start.1
  220.1 7.0 collective-permute-start.2
  251.2 5.4 conditional.3
  266.7 7.0 collective-permute-start
  275.6 7.0 collective-permute-start.1
  284.6 7.0 collective-permute-start.2
  294.0 4.8 all-to-all-start
  325.7 7.0 collective-permute-start
  334.6 7.0 collective-permute-start.1
  343.6 7.0 collective-permute-start.2
  374.7 5.5 conditional.3
  390.2 7.0 collective-permute-start
  399.1 7.0 collective-permute-start.1
  408.0 7.0 collective-permute-start.2
  449.1 7.0 collective-permute-start
  458.1 7.0 collective-permute-start.1
  467.0 7.0 collective-permute-start.2
  488.8 4.8 all-to-all-start.1
  508.1 7.0 collective-permute-start
  517.1 7.0 collective-permute-start.1
  526.0 7.0 collective-permute-start.2
  547.8 4.8 all-to-all-start.1
  567.1 7.0 collective-permute-start
  576.1 7.0 collective-permute-start.1
  585.0 7.0 collective-permute-start.2
  606.8 4.8 all-to-all-start.1
  626.1 7.0 collective-permute-start
  635.1 7.0 collective-permute-start.1
  644.0 7.0 collective-permute-start.2
  665.8 4.8 all-to-all-start.1
  685.1 7.0 collective-permute-start
  694.1 7.0 collective-permute-start.1
  703.0 7.0 collective-permute-start.2
  724.8 4.8 all-to-all-start.1
  744.1 7.0 collective-permute-start
  753.1 7.0 collective-permute-start.1
  762.0 7.0 collective-permute-start.2
  783.8 4.8 all-to-all-start.1
  793.1 5.5 conditional.3
  808.6 7.0 collective-permute-start
  817.5 7.0 collective-permute-start.1
  826.4 7.0 collective-permute-start.2
  867.6 7.0 collective-permute-start
  876.5 7.0 collective-permute-start.1
  885.4 7.0 collective-permute-start.2
  926.6 7.0 collective-permute-start
  935.5 7.0 collective-permute-start.1
  944.4 7.0 collective-permute-start.2
  975.5 5.5 conditional.3
  (825 shorter events, 537.1 us)
Async XLA Ops:
  11.5 15.2 %collective-permute-start.3 = (f32[81,64]{0,1:T(8,128)S(1)}, f32[81,64]{0,1:T(8,128)S(1)}, u32[]{:S(2)}, u32[]{:S(2)}) collective-permute-start(f32[81,64]{0,1:T(8,128)S(1)} %maximum_select_fusion.2), channel_id=1, source_target_pairs={{0,4},{4,8},{8,12},{12,16},{16,20},{20,24},{24,28},{28,32},{32,36}... | collective-permute-start | bytes 62216 | tf_op jit(solution)/shard_map/while/body/eval_jaxpr/ppermute | solution.py:13
  13.5 15.2 %collective-permute-start = (f32[81,64]{0,1:T(8,128)S(1)}, f32[81,64]{0,1:T(8,128)S(1)}, u32[]{:S(2)}, u32[]{:S(2)}) collective-permute-start(f32[81,64]{0,1:T(8,128)S(1)} %maximum_select_fusion.2), channel_id=1, source_target_pairs={{0,508},{4,0},{8,4},{12,8},{16,12},{20,16},{24,20},{28,24},{32,28}... | collective-permute-start | bytes 62216 | tf_op jit(solution)/shard_map/while/body/eval_jaxpr/ppermute | solution.py:13
  26.8 8.9 collective-permute-start.4
  28.7 8.9 collective-permute-start.1
  35.7 9.7 collective-permute-start.5
  47.1 9.3 all-to-all-start
  59.5 9.3 all-to-all-start.1
  78.9 8.9 collective-permute-start
  85.8 8.9 collective-permute-start.4
  87.8 8.9 collective-permute-start.1
  94.8 9.7 collective-permute-start.5
  106.2 9.3 all-to-all-start
  118.5 9.3 all-to-all-start.1
  143.3 8.9 collective-permute-start
  150.3 8.9 collective-permute-start.4
  152.2 8.9 collective-permute-start.1
  159.2 9.7 collective-permute-start.5
  170.6 9.3 all-to-all-start
  182.9 9.3 all-to-all-start.1
  209.3 8.9 collective-permute-start.4
  211.2 8.9 collective-permute-start.1
  218.2 9.7 collective-permute-start.5
  229.6 9.3 all-to-all-start
  241.9 9.3 all-to-all-start.1
  266.7 8.9 collective-permute-start
  273.7 8.9 collective-permute-start.4
  275.6 8.9 collective-permute-start.1
  282.6 9.7 collective-permute-start.5
  294.0 9.3 all-to-all-start
  306.3 9.3 all-to-all-start.1
  325.7 8.9 collective-permute-start
  341.6 9.7 collective-permute-start.5
  353.0 9.3 all-to-all-start
  365.3 9.3 all-to-all-start.1
  406.1 9.7 collective-permute-start.5
  417.5 9.3 all-to-all-start
  429.8 9.3 all-to-all-start.1
  465.0 9.7 collective-permute-start.5
  476.5 9.3 all-to-all-start
  488.8 9.3 all-to-all-start.1
  524.0 9.7 collective-permute-start.5
  535.5 9.3 all-to-all-start
  547.8 9.3 all-to-all-start.1
  583.0 9.7 collective-permute-start.5
  594.5 9.3 all-to-all-start
  606.8 9.3 all-to-all-start.1
  642.0 9.7 collective-permute-start.5
  653.5 9.3 all-to-all-start
  665.8 9.3 all-to-all-start.1
  701.0 9.7 collective-permute-start.5
  712.5 9.3 all-to-all-start
  724.8 9.3 all-to-all-start.1
  760.0 9.7 collective-permute-start.5
  771.5 9.3 all-to-all-start
  783.8 9.3 all-to-all-start.1
  824.5 9.7 collective-permute-start.5
  835.9 9.3 all-to-all-start
  848.2 9.3 all-to-all-start.1
  883.5 9.7 collective-permute-start.5
  894.9 9.3 all-to-all-start
  907.2 9.3 all-to-all-start.1
  942.5 9.7 collective-permute-start.5
  953.9 9.3 all-to-all-start
  966.2 9.3 all-to-all-start.1
  (65 other events, 565.3 us)
